TPU v7x, 128 devices: a whole 4x4x4 slice. The times are simulated.
128 devices in a mesh: dp: 8 (over x, z_lo), tensor: 16 (over y, z_hi, core).
Axes of the slice: x: 4, y: 4, z: 4 (z_hi: 2, z_lo: 2; z = z_hi * 2 + z_lo), core: 2. Of those that a mesh axis runs over, the one named last changes fastest.
Arguments:
- hidden_act: bfloat16 [5632, 36864], P('dp', 'tensor'), may hold values from -80 to 80
- out_grad: bfloat16 [5632, 4608], P('dp', 'tensor'), may hold values from -0.5 to 0.5
- other_sq: float32 [16], P('dp'), may hold values from 2989699 to 597939968
Outputs:
- weight_grad: float32 [4608, 36864], P('dp', 'tensor')
All inputs are finite; a program needn't handle non-finite values.
Results may differ from a plain program's by a relative error of at most 0.002.
Values may be sent and summed in bfloat16 or wider, within the bound.
A program may use at most 128 MiB of HBM per device.

v0:
```python
import math
import jax
import jax.numpy as jnp
from jax import lax
from jax.sharding import Mesh
from jax.sharding import PartitionSpec as P

D = 4608
FF = 36864
L = 352
DP = ("dp_0", "dp_1")


def in_blocks(array, dim, length):
    dims = array.shape
    blocks = array.reshape(*dims[:dim], length, dims[dim] // length, *dims[dim + 1 :])
    return jnp.moveaxis(blocks, dim, 0)


def sum_at_owner(array, axis, dim):
    length = lax.axis_size(axis)
    blocks = lax.all_to_all(in_blocks(array, dim, length), axis, 0, 0, tiled=True)
    return jnp.sum(blocks, axis=0)


def sent_to_all(array, axis):
    length = lax.axis_size(axis)
    return lax.all_to_all(
        jnp.broadcast_to(array[None], (length, *array.shape)), axis, 0, 0, tiled=True
    )


def over_copies(array, axis):
    everything = sent_to_all(array, axis)
    return jnp.sum(everything, axis=0)


def summed_rows(subtotal, axes):
    for axis in axes:
        subtotal = lax.psum_scatter(subtotal, axis, scatter_dimension=0, tiled=True)
    return subtotal


def on_device(hidden_act, out_grad, other_sq):
    examples_here = other_sq.shape[0]
    length = hidden_act.shape[0] // examples_here
    hidden_blocks = hidden_act.reshape(examples_here, length, hidden_act.shape[1])
    act_gram = jnp.einsum(
        "etf,esf->ets", hidden_blocks, hidden_blocks, preferred_element_type=jnp.float32
    )
    full_grad = lax.all_gather(out_grad, "tensor", axis=1, tiled=True)
    grad_blocks = full_grad.reshape(examples_here, length, full_grad.shape[1])
    act_share = sum_at_owner(act_gram, "tensor", 1)
    share_rows = act_share.shape[1]
    row_start = lax.axis_index("tensor") * share_rows
    grad_share = lax.dynamic_slice_in_dim(grad_blocks, row_start, share_rows, 1)
    grad_gram_rows = jnp.einsum(
        "etd,esd->ets", grad_share, grad_blocks, preferred_element_type=jnp.float32
    )
    layer_sq = over_copies(jnp.sum(act_share * grad_gram_rows, axis=(1, 2)), "tensor")
    clip_bound = math.sqrt(L * FF * D / 80.0)
    clip_scale = jnp.minimum(1.0, clip_bound / jnp.sqrt(other_sq + layer_sq))
    scaled_grad = (grad_blocks.astype(jnp.float32) * clip_scale[:, None, None]).astype(jnp.bfloat16)
    scaled_grad = scaled_grad.reshape(examples_here * length, full_grad.shape[1])
    contract_rows = (((0,), (0,)), ((), ()))
    return summed_rows(
        lax.dot_general(scaled_grad, hidden_act, contract_rows, preferred_element_type=jnp.float32),
        DP,
    )


def solution(mesh):
    torus = Mesh(mesh.devices.reshape(4, 2, mesh.shape["tensor"]), ("dp_0", "dp_1", "tensor"))
    in_specs = (P(DP, "tensor"), P(DP, "tensor"), P(DP))
    out_specs = P(DP, "tensor")
    return jax.shard_map(
        on_device, mesh=torus, in_specs=in_specs, out_specs=out_specs, check_vma=False
    )
```

profile of v0, /device:TPU:1, one launch (start us, length us, event | category | flops | bytes accessed | tf_op | source)
XLA Modules:
  0.0 625.2 jit_solution(8400824350638153253)
XLA Ops:
  6.5 0.0 copy-start
  6.5 0.0 all-gather.2.cloned.1.call-start
  6.5 0.7 all-gather.2.cloned.1.call-update
  7.3 1.2 copy-done
  8.5 1.8 fusion.5
  10.3 1.8 copy.13
  12.1 9.3 %all-to-all-start = ((f32[16,2,22,352]{3,1,2,0:T(2,128)}), f32[16,2,22,352]{3,1,2,0:T(2,128)}, u32[]{:S(2)}, u32[]{:S(2)}) async-start(f32[16,2,22,352]{3,1,2,0:T(2,128)} %bitcast.11), calls=%async_computation | async-start | bytes 2162688 | tf_op jit(solution)/shard_map/all_to_all | solution.py:22
  21.4 0.0 reduce-scatter.3.cloned.1.call-start
  21.4 20.4 %all-to-all-done = f32[16,2,22,352]{3,1,2,0:T(2,128)} async-done(((f32[16,2,22,352]{3,1,2,0:T(2,128)}), f32[16,2,22,352]{3,1,2,0:T(2,128)}, u32[]{:S(2)}, u32[]{:S(2)}) %all-to-all-start) | async-done | bytes 991264 | tf_op jit(solution)/shard_map/all_to_all | solution.py:22
  41.8 1.6 reduce_sum.27
  43.5 44.9 %all-gather.2.cloned.1.call-done = bf16[704,4608]{0,1:T(8,128)(2,1)} async-done(((bf16[704,288]{0,1:T(8,128)(2,1)}), bf16[704,4608]{0,1:T(8,128)(2,1)}) %all-gather.2.cloned.1.call-update) | async-done | bytes 6488080 | tf_op jit(solution)/shard_map/all_gather | solution.py:51
  88.4 9.4 %copy.14 = bf16[704,4608]{1,0:T(8,128)(2,1)} copy(bf16[704,4608]{0,1:T(8,128)(2,1)} %all-gather.2.cloned.1.call-done) | data formatting | bytes 12976128 | tf_op jit(solution)/shard_map/all_gather | solution.py:51
  97.8 0.0 copy-start.2
  97.8 4.9 fusion.2
  102.8 10.1 %all_to_all.11 = f32[16,1,2]{2,1,0:T(1,128)S(1)} all-to-all(f32[16,1,2]{2,1,0:T(1,128)S(1)} %broadcast_in_dim.2), channel_id=1, replica_groups=mesh['dp_0'=4,'dp_1'=2,'tensor'=16] {'tensor'}, dimensions={0} | all-to-all | bytes 256 | tf_op jit(solution)/shard_map/all_to_all | solution.py:28
  113.0 0.0 copy-done.2
  113.0 0.1 mul.21
  113.0 0.1 mul.22
  113.1 25.2 %fusion = f32[4608,2304]{1,0:T(8,128)} fusion(bf16[704,2304]{1,0:T(8,128)(2,1)S(1)} %copy-done, bf16[704,4608]{0,1:T(8,128)(2,1)} %all-gather.2.cloned.1.call-done, f32[704]{0:T(1024)S(1)} %mul.22), kind=kOutput, calls=%fused_computation.1 | convolution fusion | flops 14958231552 | bytes 52202240 | tf_op jit(solution)/shard_map/dot_general | solution.py:67
  138.4 0.0 reduce-scatter.3.cloned.1.call-update
  138.4 0.0 copy-start.1
  138.4 0.0 reduce-scatter.5.cloned.1.call-start
  138.4 352.2 %reduce-scatter.3.cloned.1.call-done = f32[1152,2304]{1,0:T(8,128)} async-done(((f32[4608,2304]{1,0:T(8,128)}), f32[1152,2304]{1,0:T(8,128)}) %reduce-scatter.3.cloned.1.call-update) | async-done | bytes 10616848 | tf_op jit(solution)/shard_map/reduce_scatter | solution.py:40
  490.6 0.0 reduce-scatter.5.cloned.1.call-update
  490.6 128.0 %reduce-scatter.5.cloned.1.call-done = f32[576,2304]{1,0:T(8,128)} async-done(((f32[1152,2304]{1,0:T(8,128)}), f32[576,2304]{1,0:T(8,128)}) %reduce-scatter.5.cloned.1.call-update) | async-done | bytes 5308432 | tf_op jit(solution)/shard_map/reduce_scatter | solution.py:40
  618.7 0.0 copy-done.1
  (3 shorter events, 0.1 us)
Async XLA Ops:
  6.5 1.9 copy-start
  6.5 81.9 %all-gather.2.cloned.1.call-start = ((), (), s32[]{:S(2)}) async-start(), calls=%async_computation.4 | async-start | bytes 7520256 | tf_op jit(solution)/shard_map/all_gather | solution.py:51
  12.1 29.7 %all-to-all-start = ((f32[16,2,22,352]{3,1,2,0:T(2,128)}), f32[16,2,22,352]{3,1,2,0:T(2,128)}, u32[]{:S(2)}, u32[]{:S(2)}) async-start(f32[16,2,22,352]{3,1,2,0:T(2,128)} %bitcast.11), calls=%async_computation | async-start | bytes 2162688 | tf_op jit(solution)/shard_map/all_to_all | solution.py:22
  21.4 469.2 %reduce-scatter.3.cloned.1.call-start = ((), (), s32[]{:S(2)}) async-start(), calls=%async_computation.5 | async-start | bytes 53084160 | tf_op jit(solution)/shard_map/reduce_scatter | solution.py:40
  97.8 15.1 %copy-start.2 = (f32[2]{0:T(128)S(1)}, f32[2]{0:T(128)}, u32[]{:S(2)}) copy-start(f32[2]{0:T(128)} %param.5) | copy-start | bytes 28
  138.4 480.3 %copy-start.1 = (bf16[704,2304]{1,0:T(8,128)(2,1)S(1)}, bf16[704,2304]{1,0:T(8,128)(2,1)}, u32[]{:S(2)}) copy-start(bf16[704,2304]{1,0:T(8,128)(2,1)} %param.3) | copy-start | bytes 9732100
  138.4 480.3 %reduce-scatter.5.cloned.1.call-start = ((), (), s32[]{:S(2)}) async-start(), calls=%async_computation.6 | async-start | bytes 15925248 | tf_op jit(solution)/shard_map/reduce_scatter | solution.py:40
Sparse Core Ops, SparseCore 0:
  9.7 78.6 all-gather.1
  138.5 352.0 reduce-scatter.2
  493.0 125.5 reduce-scatter.4
where the time goes:
time: 626 us; the launch traced here: 625 us
  waiting for transfers between devices  546 us (87%)
  matrix products  32 us (5%)
  between operations  13.1 us (2%)
  local copies, waits for them, and re-layouts  12.6 us (2%)
  blocking collectives  10.1 us (2%)
  starting transfers between devices  9.37 us (1%)
    reduce_scatter x2, waiting for transfers between devices, summed_rows(): subtotal = lax.psum_scatter(subtotal, axis, scatter_dimension=0, tiled=True)  480 us
    all_gather x1, waiting for transfers between devices, on_device(): full_grad = lax.all_gather(out_grad, 'tensor', axis=1, tiled=True)  44.9 us
    dot_general x1, matrix products, on_device(): lax.dot_general(scaled_grad, hidden_act, contract_rows, preferred_element...  25.2 us
    all_to_all x1, waiting for transfers between devices, sum_at_owner(): lax.all_to_all(in_blocks(array, dim, length), axis, 0, 0, tiled=True)  20.4 us
  transfers between devices with their start and end apart: 4, of which 4 were waited for; matrix products, arithmetic and copies ran while one was open for 1% of the time, Pallas kernels for 0%

commit v1 on v0

--- a/solution.py
+++ b/solution.py
@@ -48,7 +48,8 @@
     act_gram = jnp.einsum(
         "etf,esf->ets", hidden_blocks, hidden_blocks, preferred_element_type=jnp.float32
     )
-    full_grad = lax.all_gather(out_grad, "tensor", axis=1, tiled=True)
+    sent = jnp.stack([out_grad] * lax.axis_size("tensor"))
+    full_grad = jnp.concatenate(lax.all_to_all(sent, "tensor", 0, 0), axis=1)
     grad_blocks = full_grad.reshape(examples_here, length, full_grad.shape[1])
     act_share = sum_at_owner(act_gram, "tensor", 1)
     share_rows = act_share.shape[1]

time: 626 us -> 724 us (1.16)
  waiting for transfers between devices: 546 us -> 585 us
  blocking collectives: 10.1 us -> 45.6 us
  local copies, waits for them, and re-layouts: 12.6 us -> 40.9 us
    all_to_all x1, waiting for transfers between devices: 20.4 us -> 105 us  [on_device(): full_grad = jnp.concatenate(lax.all_to_all(sent, 'tensor', 0, 0), axis=1)]
    all_gather x1 -> x0, waiting for transfers between devices: 44.9 us -> none  [on_device(): full_grad = lax.all_gather(out_grad, 'tensor', axis=1, tiled=True)]
    another operation x0 -> x3, local copies, waits for them, and re-layouts: none -> 37.9 us  [the longest x2 34.3 us: on_device(): grad_blocks = full_grad.reshape(examples_here, length, full_grad.shape[1])]
    all_to_all x0 -> x1, blocking collectives: none -> 27.3 us  [sum_at_owner(): lax.all_to_all(in_blocks(array, dim, length), axis, 0, 0, tiled=True)]
    all_gather x1 -> x0, local copies, waits for them, and re-layouts: 9.44 us -> none  [on_device(): full_grad = lax.all_gather(out_grad, 'tensor', axis=1, tiled=True)]
    all_to_all x1, blocking collectives: 10.1 us -> 18.3 us  [sent_to_all(): lax.all_to_all(jnp.broadcast_to(array[None], (length, *array.shape)), axi...]
  transfers between devices with their start and end apart: 4 -> 3, of which waited for: 4 -> 3; matrix products, arithmetic and copies ran while one was open for 1% -> 0% of each run, Pallas kernels for 0% -> 0%
where the time goes in v1:
time: 724 us; the launch traced here: 723 us
  waiting for transfers between devices  585 us (81%)
  blocking collectives  45.6 us (6%)
  local copies, waits for them, and re-layouts  40.9 us (6%)
  matrix products  32 us (4%)
  between operations  13.5 us (2%)
    reduce_scatter x2, waiting for transfers between devices, summed_rows(): subtotal = lax.psum_scatter(subtotal, axis, scatter_dimension=0, tiled=True)  480 us
    all_to_all x1, waiting for transfers between devices, on_device(): full_grad = jnp.concatenate(lax.all_to_all(sent, 'tensor', 0, 0), axis=1)  105 us
    another operation x2, local copies, waits for them, and re-layouts, on_device(): grad_blocks = full_grad.reshape(examples_here, length, full_grad.shape[1])  34.3 us
    all_to_all x1, blocking collectives, sum_at_owner(): lax.all_to_all(in_blocks(array, dim, length), axis, 0, 0, tiled=True)  27.3 us
    dot_general x1, matrix products, on_device(): lax.dot_general(scaled_grad, hidden_act, contract_rows, preferred_element...  25.2 us
    all_to_all x1, blocking collectives, sent_to_all(): lax.all_to_all(jnp.broadcast_to(array[None], (length, *array.shape)), axi...  18.3 us
  transfers between devices with their start and end apart: 3, of which 3 were waited for; matrix products, arithmetic and copies ran while one was open for 0% of the time, Pallas kernels for 0%

profile of v1, /device:TPU:1, one launch (start us, length us, event | category | flops | bytes accessed | tf_op | source)
XLA Modules:
  0.0 723.2 jit_solution(10454587081359199828)
XLA Ops:
  6.5 0.0 copy-start
  6.5 1.9 copy-done
  8.5 0.0 copy-start.2
  8.5 1.8 fusion.7
  10.3 0.8 copy.16
  11.1 27.3 %all_to_all.16 = f32[16,2,22,352]{3,1,2,0:T(2,128)} all-to-all(f32[16,2,22,352]{3,1,2,0:T(2,128)S(1)} %bitcast.15), channel_id=1, replica_groups=mesh['dp_0'=4,'dp_1'=2,'tensor'=16] {'tensor'}, dimensions={0} | all-to-all | bytes 1982464 | tf_op jit(solution)/shard_map/all_to_all | solution.py:22
  38.5 0.0 copy-done.2
  38.5 3.6 stack.2
  42.1 4.8 all-to-all-start
  46.9 0.0 reduce-scatter.3.cloned.1.call-start
  46.9 1.6 reduce_sum.27
  48.6 104.7 %all-to-all-done = bf16[16,704,288]{1,2,0:T(8,128)(2,1)} async-done(((bf16[16,704,288]{1,2,0:T(8,128)(2,1)}), bf16[16,704,288]{1,2,0:T(8,128)(2,1)}, u32[]{:S(2)}, u32[]{:S(2)}) %all-to-all-start) | async-done | bytes 6488096 | tf_op jit(solution)/shard_map/all_to_all | solution.py:52
  153.3 16.3 %reshape_reshape.3 = bf16[2,352,4608]{1,0,2:T(2,128)(2,1)} reshape(bf16[704,16,288]{0,2,1:T(8,128)(2,1)} %bitcast) | data formatting | bytes 12976128 | tf_op jit(solution)/shard_map/reshape;reshape | solution.py:53
  169.6 18.0 %copy.17 = bf16[2,352,4608]{2,1,0:T(8,128)(2,1)} copy(bf16[2,352,4608]{1,0,2:T(2,128)(2,1)} %reshape_reshape.3) | data formatting | bytes 12976128 | tf_op jit(solution)/shard_map/reshape;reshape | solution.py:53
  187.6 0.0 copy-start.3
  187.6 4.9 fusion.4
  192.6 18.3 %all_to_all.17 = f32[16,1,2]{2,1,0:T(1,128)S(1)} all-to-all(f32[16,1,2]{2,1,0:T(1,128)S(1)} %broadcast_in_dim.2), channel_id=1, replica_groups=mesh['dp_0'=4,'dp_1'=2,'tensor'=16] {'tensor'}, dimensions={0} | all-to-all | bytes 256 | tf_op jit(solution)/shard_map/all_to_all | solution.py:28
  210.9 0.0 copy-done.3
  210.9 0.1 mul.21
  211.0 0.1 mul.22
  211.1 25.2 %fusion.1 = f32[4608,2304]{1,0:T(8,128)} fusion(bf16[704,2304]{1,0:T(8,128)(2,1)S(1)} %copy-done, bf16[704,4608]{0,1:T(8,128)(2,1)} %bitcast.5, f32[704]{0:T(1024)S(1)} %mul.22), kind=kOutput, calls=%fused_computation.2 | convolution fusion | flops 14958231552 | bytes 52202240 | tf_op jit(solution)/shard_map/dot_general | solution.py:68
  236.3 0.0 reduce-scatter.3.cloned.1.call-update
  236.3 0.0 copy-start.1
  236.3 0.0 reduce-scatter.5.cloned.1.call-start
  236.4 351.9 %reduce-scatter.3.cloned.1.call-done = f32[1152,2304]{1,0:T(8,128)} async-done(((f32[4608,2304]{1,0:T(8,128)}), f32[1152,2304]{1,0:T(8,128)}) %reduce-scatter.3.cloned.1.call-update) | async-done | bytes 10616848 | tf_op jit(solution)/shard_map/reduce_scatter | solution.py:40
  588.3 0.0 reduce-scatter.5.cloned.1.call-update
  588.3 128.0 %reduce-scatter.5.cloned.1.call-done = f32[576,2304]{1,0:T(8,128)} async-done(((f32[1152,2304]{1,0:T(8,128)}), f32[576,2304]{1,0:T(8,128)}) %reduce-scatter.5.cloned.1.call-update) | async-done | bytes 5308432 | tf_op jit(solution)/shard_map/reduce_scatter | solution.py:40
  716.3 0.0 copy-done.1
  (3 shorter events, 0.1 us)
Async XLA Ops:
  6.5 1.9 copy-start
  8.5 30.0 %copy-start.2 = (bf16[704,288]{0,1:T(8,128)(2,1)S(1)}, bf16[704,288]{0,1:T(8,128)(2,1)}, u32[]{:S(2)}) copy-start(bf16[704,288]{0,1:T(8,128)(2,1)} %param.4) | copy-start | bytes 1216516
  42.1 111.2 %all-to-all-start = ((bf16[16,704,288]{1,2,0:T(8,128)(2,1)}), bf16[16,704,288]{1,2,0:T(8,128)(2,1)}, u32[]{:S(2)}, u32[]{:S(2)}) async-start(bf16[16,704,288]{1,2,0:T(8,128)(2,1)} %stack.2), calls=%async_computation | async-start | bytes 14155776 | tf_op jit(solution)/shard_map/all_to_all | solution.py:52
  46.9 541.4 %reduce-scatter.3.cloned.1.call-start = ((), (), s32[]{:S(2)}) async-start(), calls=%async_computation.5 | async-start | bytes 53084160 | tf_op jit(solution)/shard_map/reduce_scatter | solution.py:40
  187.6 23.3 %copy-start.3 = (f32[2]{0:T(128)S(1)}, f32[2]{0:T(128)}, u32[]{:S(2)}) copy-start(f32[2]{0:T(128)} %param.5) | copy-start | bytes 28
  236.3 480.0 %copy-start.1 = (bf16[704,2304]{1,0:T(8,128)(2,1)S(1)}, bf16[704,2304]{1,0:T(8,128)(2,1)}, u32[]{:S(2)}) copy-start(bf16[704,2304]{1,0:T(8,128)(2,1)} %param.3) | copy-start | bytes 9732100
  236.3 480.0 %reduce-scatter.5.cloned.1.call-start = ((), (), s32[]{:S(2)}) async-start(), calls=%async_computation.6 | async-start | bytes 15925248 | tf_op jit(solution)/shard_map/reduce_scatter | solution.py:40
Sparse Core Ops, SparseCore 0:
  236.4 351.7 reduce-scatter.2
  590.7 125.6 reduce-scatter.4
